TPU v7x, 512 devices: a whole 4x4x16 slice. The times are simulated.
512 devices in a mesh: expert: 32 (over z_lo, x, core), fsdp: 4 (over z_hi), dp: 4 (over y).
Axes of the slice: x: 4, y: 4, z: 16 (z_hi: 4, z_lo: 4; z = z_hi * 4 + z_lo), core: 2. Of those that a mesh axis runs over, the one named last changes fastest.
Arguments:
- tokens: bfloat16 [8192, 3584], P(('expert', 'fsdp', 'dp')), may hold values from -6 to 6
- routes: int32 [8192, 3], P(('expert', 'fsdp', 'dp')), may hold values from 0 to 31, all different within a row; in each aligned block of 16 rows (0 to 15, 16 to 31, ...) at most 2 rows name the same one
- gate_fixed: int32 [8192, 3], P(('expert', 'fsdp', 'dp')), may hold values from 1 to 65535
- gate_weight: bfloat16 [32, 3584, 1024], P('expert', 'fsdp', 'dp'), may hold values from -0.09375 to 0.09375
- up_weight: bfloat16 [32, 3584, 1024], P('expert', 'fsdp', 'dp'), may hold values from -0.09375 to 0.09375
- down_weight: bfloat16 [32, 1024, 3584], P('expert', 'dp', 'fsdp'), may hold values from -0.1875 to 0.1875
- cotangent: bfloat16 [8192, 3584], P(('expert', 'fsdp', 'dp')), may hold values from -24 to 24
Outputs:
- mixed: bfloat16 [8192, 3584], P(('expert', 'fsdp', 'dp'))
- grad_tokens: bfloat16 [8192, 3584], P(('expert', 'fsdp', 'dp'))
- grad_down: float32 [32, 1024, 3584], P('expert', 'dp', 'fsdp')
- grad_gate: float32 [32, 3584, 1024], P('expert', 'fsdp', 'dp')
- grad_up: float32 [32, 3584, 1024], P('expert', 'fsdp', 'dp')
Inputs may be any that keep to these rules, and one draw needn't show every extreme that they name: `routes`: each row names 3 different experts; the 16 rows of one device name any one expert at most 2 times, and in every draw some device names some expert exactly 2 times.
All inputs are finite; a program needn't handle non-finite values.
Results may differ from a plain program's by a relative error of at most 0.0064.
Values may be sent and summed in bfloat16 or wider, within the bound.
A program may use at most 64 MiB of HBM per device.

v0:
```python
import jax
import jax.numpy as jnp
from jax import lax
from jax.sharding import PartitionSpec as P


def deliver(buffer, expert_count, group_count, capacity):
    columns = buffer.shape[1]
    spread = jnp.broadcast_to(
        buffer.reshape(expert_count, 1, capacity, columns),
        (expert_count, group_count, capacity, columns),
    )
    arrived = lax.all_to_all(
        spread.reshape(expert_count * group_count, capacity, columns),
        ("expert", "dp"),
        split_axis=0,
        concat_axis=0,
        tiled=True,
    )
    return arrived.reshape(expert_count * group_count * capacity, columns)


def send_home(partial_value, expert_count, group_count, capacity):
    columns = partial_value.shape[1]
    blocks = partial_value.reshape(expert_count, group_count, capacity, columns)
    returned = lax.all_to_all(
        blocks.reshape(expert_count * group_count, capacity, columns),
        ("expert", "dp"),
        split_axis=0,
        concat_axis=0,
        tiled=True,
    )
    returned = returned.reshape(expert_count, group_count, capacity, columns)
    return jnp.sum(returned.astype(jnp.float32), axis=1).reshape(expert_count * capacity, columns)


def body(tokens, routes, gate_fixed, gate_weight, up_weight, down_weight, cotangent):
    expert_count = lax.axis_size("expert")
    group_count = lax.axis_size("dp")
    token_count, top_count = routes.shape
    capacity = max(2, -(-(token_count * top_count) // expert_count))
    slot_count = expert_count * capacity
    flat_ids = routes.reshape(token_count * top_count)
    one_hot = (flat_ids[:, None] == jnp.arange(expert_count, dtype=jnp.int32)[None, :]).astype(
        jnp.int32
    )
    running = jnp.cumsum(one_hot, axis=0)
    slot_index = jnp.sum(running * one_hot, axis=1) - 1
    destination = (flat_ids * capacity + slot_index).reshape(token_count, top_count)
    coefficient = gate_fixed.astype(jnp.float32) / 65536.0
    matched = destination[None, :, :] == jnp.arange(slot_count, dtype=jnp.int32)[:, None, None]
    selector = jnp.sum(matched.astype(jnp.float32), axis=2)
    weighted = jnp.sum(jnp.where(matched, coefficient[None, :, :], jnp.float32(0.0)), axis=2)
    gate_full, up_full, down_full = (
        lax.all_gather(gate_weight[0], "fsdp", axis=0, tiled=True),
        lax.all_gather(up_weight[0], "fsdp", axis=0, tiled=True),
        lax.all_gather(down_weight[0], "fsdp", axis=1, tiled=True),
    )
    send_rows = jnp.dot(
        selector.astype(jnp.bfloat16), tokens, preferred_element_type=jnp.float32
    ).astype(jnp.bfloat16)
    arrived_rows = deliver(send_rows, expert_count, group_count, capacity)
    gate_pre = jnp.dot(arrived_rows, gate_full, preferred_element_type=jnp.float32)
    up_pre = jnp.dot(arrived_rows, up_full, preferred_element_type=jnp.float32)
    sigmoid_gate = jax.nn.sigmoid(gate_pre)
    swish = gate_pre * sigmoid_gate
    hidden = (swish * up_pre).astype(jnp.bfloat16)
    partial_value = jnp.dot(hidden, down_full, preferred_element_type=jnp.float32).astype(
        jnp.bfloat16
    )
    summed = send_home(partial_value, expert_count, group_count, capacity)
    mixed = jnp.dot(
        weighted.T, summed, precision=lax.Precision.HIGHEST, preferred_element_type=jnp.float32
    ).astype(jnp.bfloat16)
    scaled = jnp.dot(
        weighted,
        cotangent.astype(jnp.float32),
        precision=lax.Precision.HIGHEST,
        preferred_element_type=jnp.float32,
    ).astype(jnp.bfloat16)
    grad_rows = deliver(scaled, expert_count, group_count, capacity)
    hidden_grad = jnp.einsum("rd,hd->rh", grad_rows, down_full, preferred_element_type=jnp.float32)
    gate_grad = (
        hidden_grad * up_pre * sigmoid_gate * (1.0 + gate_pre * (1.0 - sigmoid_gate))
    ).astype(jnp.bfloat16)
    up_grad = (hidden_grad * swish).astype(jnp.bfloat16)
    back = jnp.einsum("rh,dh->rd", gate_grad, gate_full, preferred_element_type=jnp.float32)
    back = back + jnp.einsum("rh,dh->rd", up_grad, up_full, preferred_element_type=jnp.float32)
    back_sum = send_home(back.astype(jnp.bfloat16), expert_count, group_count, capacity)
    grad_tokens = jnp.dot(
        selector.T, back_sum, precision=lax.Precision.HIGHEST, preferred_element_type=jnp.float32
    ).astype(jnp.bfloat16)
    row_cols = lax.all_to_all(arrived_rows, "fsdp", split_axis=1, concat_axis=0, tiled=True)
    gate_all, up_all = (
        lax.all_gather(gate_grad, "fsdp", axis=0, tiled=True),
        lax.all_gather(up_grad, "fsdp", axis=0, tiled=True),
    )
    down_term = jnp.einsum("rh,rd->hd", hidden, grad_rows, preferred_element_type=jnp.float32)
    grad_down = lax.psum_scatter(down_term, "fsdp", scatter_dimension=1, tiled=True)
    grad_gate = jnp.einsum("rd,rh->dh", row_cols, gate_all, preferred_element_type=jnp.float32)
    grad_up = jnp.einsum("rd,rh->dh", row_cols, up_all, preferred_element_type=jnp.float32)
    return (mixed, grad_tokens, grad_down[None], grad_gate[None], grad_up[None])


def solution(mesh):
    placed = (
        P(("expert", "fsdp", "dp"), None),
        P(("expert", "fsdp", "dp"), None),
        P(("expert", "fsdp", "dp"), None),
        P("expert", "fsdp", "dp"),
        P("expert", "fsdp", "dp"),
        P("expert", "dp", "fsdp"),
        P(("expert", "fsdp", "dp"), None),
    )
    return jax.shard_map(
        body,
        mesh=mesh,
        in_specs=placed,
        out_specs=(
            P(("expert", "fsdp", "dp"), None),
            P(("expert", "fsdp", "dp"), None),
            P("expert", "dp", "fsdp"),
            P("expert", "fsdp", "dp"),
            P("expert", "fsdp", "dp"),
        ),
        check_vma=False,
    )
```

profile of v0, /device:TPU:72, one launch (start us, length us, event | category | flops | bytes accessed | tf_op | source)
XLA Modules:
  0.0 713.5 jit_solution(12162136973286649150)
XLA Ops:
  10.5 2.2 broadcast_in_dim.41
  12.7 12.3 %all-to-all-start = ((bf16[128,2,3584]{2,1,0:T(2,128)(2,1)}), bf16[128,2,3584]{2,1,0:T(2,128)(2,1)S(1)}, u32[]{:S(2)}, u32[]{:S(2)}) async-start(bf16[128,2,3584]{2,1,0:T(2,128)(2,1)} %bitcast.53), calls=%async_computation | async-start | bytes 3670016 | tf_op jit(solution)/shard_map/all_to_all | solution.py:13
  25.8 41.1 %all-to-all-done = bf16[128,2,3584]{2,1,0:T(2,128)(2,1)S(1)} async-done(((bf16[128,2,3584]{2,1,0:T(2,128)(2,1)}), bf16[128,2,3584]{2,1,0:T(2,128)(2,1)S(1)}, u32[]{:S(2)}, u32[]{:S(2)}) %all-to-all-start) | async-done | bytes 1835040 | tf_op jit(solution)/shard_map/all_to_all | solution.py:13
  66.9 2.2 broadcast_in_dim.43
  69.2 11.7 %all-to-all-start.2 = ((bf16[128,2,3584]{2,1,0:T(2,128)(2,1)}), bf16[128,2,3584]{2,1,0:T(2,128)(2,1)}, u32[]{:S(2)}, u32[]{:S(2)}) async-start(bf16[128,2,3584]{2,1,0:T(2,128)(2,1)} %bitcast.52), calls=%async_computation.2 | async-start | bytes 3670016 | tf_op jit(solution)/shard_map/all_to_all | solution.py:13
  82.4 2.1 all_to_all.30
  84.5 2.9 copy.32
  87.5 90.4 %all-to-all-done.2 = bf16[128,2,3584]{2,1,0:T(2,128)(2,1)} async-done(((bf16[128,2,3584]{2,1,0:T(2,128)(2,1)}), bf16[128,2,3584]{2,1,0:T(2,128)(2,1)}, u32[]{:S(2)}, u32[]{:S(2)}) %all-to-all-start.2) | async-done | bytes 1835040 | tf_op jit(solution)/shard_map/all_to_all | solution.py:13
  177.8 12.6 %all-to-all-start.4 = ((bf16[256,4,896]{2,0,1:T(8,128)(2,1)}), bf16[256,4,896]{2,0,1:T(8,128)(2,1)}, u32[]{:S(2)}, u32[]{:S(2)}) async-start(bf16[256,4,896]{2,0,1:T(8,128)(2,1)} %copy.32), calls=%async_computation.5 | async-start | bytes 3670016 | tf_op jit(solution)/shard_map/all_to_all | solution.py:93
  192.8 5.0 reshape.58
  197.8 2.1 fusion.9
  200.0 80.8 %all-gather.9.cloned.1.call-done = bf16[1,3584,256]{2,1,0:T(8,128)(2,1)} async-done(((bf16[1,896,256]{2,1,0:T(8,128)(2,1)}), bf16[1,3584,256]{2,1,0:T(8,128)(2,1)}) %all-gather.9.cloned.1.call-update) | async-done | bytes 1835024 | tf_op jit(solution)/shard_map/all_gather | solution.py:56
  282.9 133.5 %all-gather.11.cloned.1.call-done = bf16[1,256,3584]{2,1,0:T(8,128)(2,1)} async-done(((bf16[1,256,896]{2,1,0:T(8,128)(2,1)}), bf16[1,256,3584]{2,1,0:T(8,128)(2,1)}) %all-gather.11.cloned.1.call-update) | async-done | bytes 1835024 | tf_op jit(solution)/shard_map/all_gather | solution.py:57
  416.4 2.9 multiply_convert_fusion
  421.6 13.1 %all-to-all-start.1 = ((bf16[128,2,3584]{2,1,0:T(2,128)(2,1)}), bf16[128,2,3584]{2,1,0:T(2,128)(2,1)}, u32[]{:S(2)}, u32[]{:S(2)}) async-start(bf16[128,2,3584]{2,1,0:T(2,128)(2,1)} %reshape_reshape.6), calls=%async_computation.1 | async-start | bytes 3670016 | tf_op jit(solution)/shard_map/all_to_all | solution.py:26
  438.5 37.7 %all-to-all-done.1 = bf16[128,2,3584]{2,1,0:T(2,128)(2,1)} async-done(((bf16[128,2,3584]{2,1,0:T(2,128)(2,1)}), bf16[128,2,3584]{2,1,0:T(2,128)(2,1)}, u32[]{:S(2)}, u32[]{:S(2)}) %all-to-all-start.1) | async-done | bytes 1835040 | tf_op jit(solution)/shard_map/all_to_all | solution.py:26
  476.2 11.7 %all-to-all-start.3 = ((bf16[128,2,3584]{2,1,0:T(2,128)(2,1)}), bf16[128,2,3584]{2,1,0:T(2,128)(2,1)}, u32[]{:S(2)}, u32[]{:S(2)}) async-start(bf16[128,2,3584]{2,1,0:T(2,128)(2,1)} %reshape_reshape.7), calls=%async_computation.3 | async-start | bytes 3670016 | tf_op jit(solution)/shard_map/all_to_all | solution.py:26
  488.0 2.5 fusion.14
  490.5 177.0 %all_gather.18 = bf16[1024,256]{1,0:T(8,128)(2,1)S(1)} all-gather(bf16[256,256]{1,0:T(8,128)(2,1)S(1)} %get-tuple-element.8), channel_id=1, replica_groups=mesh['expert'=32,'fsdp'=4,'dp'=4] {'fsdp'}, dimensions={0}, use_global_device_ids=true | all-gather | bytes 655360 | tf_op jit(solution)/shard_map/all_gather | solution.py:95
  667.5 22.2 %all_gather.19 = bf16[1024,256]{1,0:T(8,128)(2,1)S(1)} all-gather(bf16[256,256]{1,0:T(8,128)(2,1)S(1)} %get-tuple-element.7), channel_id=1, replica_groups=mesh['expert'=32,'fsdp'=4,'dp'=4] {'fsdp'}, dimensions={0}, use_global_device_ids=true | all-gather | bytes 655360 | tf_op jit(solution)/shard_map/all_gather | solution.py:96
  689.7 3.1 convolution_bitcast_fusion.1
  692.8 3.1 convolution_bitcast_fusion
  695.9 3.7 convert_reduce_fusion.1
  700.3 3.7 convert_reduce_fusion
  (52 shorter events, 19.9 us)
Async XLA Ops:
  7.2 2.9 copy-start
  12.7 12.3 %copy-start.6 = (bf16[16,3584]{1,0:T(8,128)(2,1)S(1)}, bf16[16,3584]{1,0:T(8,128)(2,1)}, u32[]{:S(2)}) copy-start(bf16[16,3584]{1,0:T(8,128)(2,1)} %param.13) | copy-start | bytes 344068
  12.7 54.2 %all-to-all-start = ((bf16[128,2,3584]{2,1,0:T(2,128)(2,1)}), bf16[128,2,3584]{2,1,0:T(2,128)(2,1)S(1)}, u32[]{:S(2)}, u32[]{:S(2)}) async-start(bf16[128,2,3584]{2,1,0:T(2,128)(2,1)} %bitcast.53), calls=%async_computation | async-start | bytes 3670016 | tf_op jit(solution)/shard_map/all_to_all | solution.py:13
  69.2 108.7 %all-to-all-start.2 = ((bf16[128,2,3584]{2,1,0:T(2,128)(2,1)}), bf16[128,2,3584]{2,1,0:T(2,128)(2,1)}, u32[]{:S(2)}, u32[]{:S(2)}) async-start(bf16[128,2,3584]{2,1,0:T(2,128)(2,1)} %bitcast.52), calls=%async_computation.2 | async-start | bytes 3670016 | tf_op jit(solution)/shard_map/all_to_all | solution.py:13
  80.9 116.9 %all-gather.7.cloned.1.call-start = ((), (), s32[]{:S(2)}) async-start(), calls=%async_computation.7 | async-start | bytes 2293760 | tf_op jit(solution)/shard_map/all_gather | solution.py:55
  81.6 199.1 %all-gather.9.cloned.1.call-start = ((), (), s32[]{:S(2)}) async-start(), calls=%async_computation.8 | async-start | bytes 2293760 | tf_op jit(solution)/shard_map/all_gather | solution.py:56
  177.8 243.7 %all-to-all-start.4 = ((bf16[256,4,896]{2,0,1:T(8,128)(2,1)}), bf16[256,4,896]{2,0,1:T(8,128)(2,1)}, u32[]{:S(2)}, u32[]{:S(2)}) async-start(bf16[256,4,896]{2,0,1:T(8,128)(2,1)} %copy.32), calls=%async_computation.5 | async-start | bytes 3670016 | tf_op jit(solution)/shard_map/all_to_all | solution.py:93
  190.4 226.0 %all-gather.11.cloned.1.call-start = ((), (), s32[]{:S(2)}) async-start(), calls=%async_computation.9 | async-start | bytes 2293760 | tf_op jit(solution)/shard_map/all_gather | solution.py:57
  192.8 5.1 copy-start.1
  416.4 2.9 copy-start.5
  421.6 13.1 %copy-start.4 = (bf16[1,3584,256]{2,1,0:T(8,128)(2,1)S(1)}, bf16[1,3584,256]{2,1,0:T(8,128)(2,1)}, u32[]{:S(2)}) copy-start(bf16[1,3584,256]{2,1,0:T(8,128)(2,1)} %all-gather.7.cloned.1.call-done) | copy-start | bytes 5505028
  421.6 54.6 %all-to-all-start.1 = ((bf16[128,2,3584]{2,1,0:T(2,128)(2,1)}), bf16[128,2,3584]{2,1,0:T(2,128)(2,1)}, u32[]{:S(2)}, u32[]{:S(2)}) async-start(bf16[128,2,3584]{2,1,0:T(2,128)(2,1)} %reshape_reshape.6), calls=%async_computation.1 | async-start | bytes 3670016 | tf_op jit(solution)/shard_map/all_to_all | solution.py:26
  434.7 1.5 copy-start.2
  438.5 49.5 %copy-start.3 = (bf16[256,3584]{1,0:T(8,128)(2,1)S(1)}, bf16[256,3584]{1,0:T(8,128)(2,1)}, u32[]{:S(2)}) copy-start(bf16[256,3584]{1,0:T(8,128)(2,1)} %reshape.58) | copy-start | bytes 5505028
  476.2 224.0 %all-to-all-start.3 = ((bf16[128,2,3584]{2,1,0:T(2,128)(2,1)}), bf16[128,2,3584]{2,1,0:T(2,128)(2,1)}, u32[]{:S(2)}, u32[]{:S(2)}) async-start(bf16[128,2,3584]{2,1,0:T(2,128)(2,1)} %reshape_reshape.7), calls=%async_computation.3 | async-start | bytes 3670016 | tf_op jit(solution)/shard_map/all_to_all | solution.py:26
  488.0 219.1 %reduce-scatter.2.cloned.1.call-start = ((), (), s32[]{:S(2)}) async-start(), calls=%async_computation.6 | async-start | bytes 4587520 | tf_op jit(solution)/shard_map/reduce_scatter | solution.py:99
Sparse Core Ops, SparseCore 0:
  83.8 102.7 all-gather.6
  188.8 91.9 all-gather.8
  282.8 133.4 all-gather.10
  491.9 182.6 reduce-scatter.1
where the time goes:
time: 715 us; the launch traced here: 714 us
  waiting for transfers between devices  386 us (54%)
  blocking collectives  199 us (28%)
  starting transfers between devices  61.6 us (9%)
  local copies, waits for them, and re-layouts  23 us (3%)
  matrix products  21.1 us (3%)
  between operations  14 us (2%)
  other arithmetic  9.2 us (1%)
    all_gather x1, blocking collectives, body(): lax.all_gather(gate_grad, 'fsdp', axis=0, tiled=True)  177 us
    all_gather x1, waiting for transfers between devices, body(): lax.all_gather(down_weight[0], 'fsdp', axis=1, tiled=True)  134 us
    all_to_all x2, waiting for transfers between devices, deliver(): lax.all_to_all(spread.reshape(expert_count * group_count, capacity, colum...  131 us
    all_gather x1, waiting for transfers between devices, body(): lax.all_gather(up_weight[0], 'fsdp', axis=0, tiled=True)  80.8 us
    all_to_all x2, waiting for transfers between devices, send_home(): lax.all_to_all(blocks.reshape(expert_count * group_count, capacity, colum...  37.7 us
    all_to_all x2, starting transfers between devices, send_home(): lax.all_to_all(blocks.reshape(expert_count * group_count, capacity, colum...  24.8 us
    all_to_all x2, starting transfers between devices, deliver(): lax.all_to_all(spread.reshape(expert_count * group_count, capacity, colum...  24.1 us
    all_gather x1, blocking collectives, body(): lax.all_gather(up_grad, 'fsdp', axis=0, tiled=True)  22.2 us
  transfers between devices with their start and end apart: 9, of which 5 were waited for; matrix products, arithmetic and copies ran while one was open for 6% of the time, Pallas kernels for 0%

commit v1 on v0

v1 whole, which is shorter than its diff:
```python
import functools

import jax
import jax.numpy as jnp
from jax import lax
from jax.experimental import pallas as pl
from jax.experimental.pallas import tpu as pltpu
from jax.sharding import PartitionSpec as P

F32 = jnp.float32
BF16 = jnp.bfloat16
CAP = 2


def log2(number):
    assert number & (number - 1) == 0
    return number.bit_length() - 1


def dot(a, b, ca, cb):
    return lax.dot_general(a, b, (((ca,), (cb,)), ((), ())), preferred_element_type=F32)


def kernel(
    sizes,
    tok_ref, cot_ref, routes_ref, fixed_ref, wg_ref, wu_ref, wd_ref,
    mixed_ref, gtok_ref, gdown_ref, ggate_ref, gup_ref,
    info, xb, xs, xe, pf, rss, rsr, agb, hs, hr, own, isb, irb, mp, ks, kr, ls, lr, w_hi, w_lo, w_one,
    sa, ra, sai, rai, sb, rb, sbi, rbi, sd, rd, se, re, sr, rr, sg, rg, sh, rh, si, ri, sk, rk, sl, rl,
):
    n_zl, n_xc, n_f, n_d = sizes
    n_tok, top = routes_ref.shape
    cols = wg_ref.shape[0]
    hid = wg_ref.shape[1]
    n_src = n_zl * n_f
    col_tok = n_src * n_tok
    slots = n_xc * n_src * CAP
    rows = slots
    part = rows // n_f

    e = lax.axis_index("expert")
    f = lax.axis_index("fsdp")
    d = lax.axis_index("dp")
    zl = e // n_xc
    xc = e % n_xc

    def at_f(j):
        return (f + j) % n_f

    def at_z(j):
        return (zl + j) % n_zl

    def at_x(j):
        return (xc + j) % n_xc

    def at_d(j):
        return (d + j) % n_d

    def device(zl_to=zl, xc_to=xc, f_to=f, d_to=d):
        return {"expert": zl_to * n_xc + xc_to, "fsdp": f_to, "dp": d_to}

    def copy(src, dst, send, recv, **to):
        return pltpu.make_async_remote_copy(
            src_ref=src,
            dst_ref=dst,
            send_sem=send,
            recv_sem=recv,
            device_id=device(**to),
            device_id_type=pl.DeviceIdType.MESH,
        )

    barrier = pltpu.get_barrier_semaphore()
    count = 0
    for limit, name, at in ((n_f, "f_to", at_f), (n_zl, "zl_to", at_z), (n_xc, "xc_to", at_x), (n_d, "d_to", at_d)):
        for j in range(1, limit):
            pl.semaphore_signal(
                barrier, inc=1, device_id=device(**{name: at(j)}), device_id_type=pl.DeviceIdType.MESH
            )
            count += 1

    lane = lax.broadcasted_iota(jnp.int32, (n_tok, 128), 1)
    packed = jnp.zeros((n_tok, 128), jnp.int32)
    for k in range(top):
        packed = jnp.where(lane == k, routes_ref[:, k : k + 1], packed)
        packed = jnp.where(lane == top + k, fixed_ref[:, k : k + 1], packed)
    info[zl, f] = packed
    own_cols = pl.ds(pl.multiple_of(f * cols, 128), cols)
    xb[0, zl, f] = tok_ref[:, own_cols]
    xb[1, zl, f] = cot_ref[:, own_cols]

    pl.semaphore_wait(barrier, count)

    def copy_a(a, j):
        there = at_f(j)
        src = (tok_ref, cot_ref)[a]
        columns = pl.ds(pl.multiple_of(there * cols, 128), cols)
        return copy(src.at[:, columns], xb.at[a, zl, f], sa.at[a, j], ra.at[a, j], f_to=there)

    def copy_ai(j):
        return copy(info.at[zl, f], info.at[zl, f], sai.at[j], rai.at[j], f_to=at_f(j))

    for j in range(1, n_f):
        copy_ai(j).start()
    for a in range(2):
        for j in range(1, n_f):
            copy_a(a, j).start()

    def copy_b(a, j):
        return copy(xb.at[a, zl], xb.at[a, zl], sb.at[a, j], rb.at[a, j], zl_to=at_z(j))

    def copy_bi(j):
        return copy(info.at[zl], info.at[zl], sbi.at[j], rbi.at[j], zl_to=at_z(j))

    for j in range(1, n_f):
        copy_ai(j).wait_recv()
    for j in range(1, n_zl):
        copy_bi(j).start()
    for a in range(2):
        for j in range(1, n_f):
            copy_a(a, j).wait_recv()
        for j in range(1, n_zl):
            copy_b(a, j).start()

    for j in range(1, n_zl):
        copy_bi(j).wait_recv()
    table = info[...].reshape(col_tok, 128)
    slot = lax.broadcasted_iota(jnp.int32, (col_tok, slots), 1)
    token = lax.broadcasted_iota(jnp.int32, (col_tok, slots), 0)
    slot_expert = zl * n_xc + lax.shift_right_logical(slot, log2(n_src * CAP))
    slot_source = lax.shift_right_logical(slot, log2(CAP)) & (n_src - 1)
    slot_rank = (slot & (CAP - 1)).astype(F32)
    hit = [table[:, k : k + 1] == slot_expert for k in range(top)]
    named = functools.reduce(jnp.logical_or, hit)
    before_row = lax.broadcasted_iota(jnp.int32, (col_tok, col_tok), 0)
    before_col = lax.broadcasted_iota(jnp.int32, (col_tok, col_tok), 1)
    shift = log2(n_tok)
    earlier = (before_col < before_row) & (
        lax.shift_right_logical(before_col, shift) == lax.shift_right_logical(before_row, shift)
    )
    rank = dot(jnp.where(earlier, 1.0, 0.0).astype(BF16), jnp.where(named, 1.0, 0.0).astype(BF16), 1, 0)
    chosen = named & (rank == slot_rank) & (lax.shift_right_logical(token, shift) == slot_source)
    weight = jnp.zeros((col_tok, slots), F32)
    for k in range(top):
        value = table[:, top + k : top + k + 1].astype(F32) * (1.0 / 65536.0)
        weight = jnp.where(hit[k], value, weight)
    weight = jnp.where(chosen, weight, 0.0)
    high = weight.astype(BF16)
    w_hi[...] = high
    w_lo[...] = (weight - high.astype(F32)).astype(BF16)
    w_one[...] = jnp.where(chosen, 1.0, 0.0).astype(BF16)

    def copy_d(a, j):
        there = at_x(j)
        return copy(xs.at[a, there], xe.at[a, d, xc], sd.at[a, j], rd.at[a, j], xc_to=there)

    for a in range(2):
        for j in range(1, n_zl):
            copy_b(a, j).wait_recv()
        table_rows = xb[a].reshape(col_tok, cols)
        if a == 0:
            picked = dot(w_one[...], table_rows, 0, 0)
        else:
            picked = dot(w_hi[...], table_rows, 0, 0) + dot(w_lo[...], table_rows, 0, 0)
        xs[a] = picked.astype(BF16).reshape(n_xc, n_src * CAP, cols)
        xe[a, d, xc] = xs[a, xc]
        for j in range(1, n_xc):
            copy_d(a, j).start()

    def copy_e(a, j):
        return copy(xe.at[a, d], xe.at[a, d], se.at[a, j], re.at[a, j], d_to=at_d(j))

    for a in range(2):
        for j in range(1, n_xc):
            copy_d(a, j).wait_recv()
        for j in range(1, n_d):
            copy_e(a, j).start()

    def copy_r(k, j):
        there = at_f(j)
        return copy(rss.at[k, there], rsr.at[k, f], sr.at[k, j], rr.at[k, j], f_to=there)

    def from_d(k):
        return (d - k + n_d) % n_d

    @pl.loop(0, n_d)
    def _(k):
        chunk = from_d(k)

        @pl.when(k > 0)
        def _():
            for a in range(2):
                copy_e(a, k).wait_recv()

        x_rows = xe[0, chunk].reshape(rows, cols)
        pf[k, :, :hid] = dot(x_rows, wg_ref[...], 1, 0)
        pf[k, :, hid : 2 * hid] = dot(x_rows, wu_ref[...], 1, 0)
        pf[k, :, 2 * hid :] = dot(xe[1, chunk].reshape(rows, cols), wd_ref[...], 1, 1)
        rss[k] = pf[k].astype(BF16).reshape(n_f, part, 3 * hid)
        for j in range(1, n_f):
            copy_r(k, j).start()

    def copy_g(k, j):
        mine = agb.at[from_d(k), f]
        return copy(mine, mine, sg.at[k, j], rg.at[k, j], f_to=at_f(j))

    @pl.loop(0, n_d)
    def _(i):
        k = (i + 1) % n_d
        for j in range(1, n_f):
            copy_r(k, j).wait_recv()
        total = pf[k, pl.ds(pl.multiple_of(f * part, part), part), :]
        for j in range(1, n_f):
            total = total + rsr[k, at_f(j)].astype(F32)
        gate, up, grad = total[:, :hid], total[:, hid : 2 * hid], total[:, 2 * hid :]
        sigmoid = jax.nn.sigmoid(gate)
        swish = gate * sigmoid
        chunk = from_d(k)
        agb[chunk, f, :, :hid] = (swish * up).astype(BF16)
        agb[chunk, f, :, hid : 2 * hid] = (grad * up * sigmoid * (1.0 + gate * (1.0 - sigmoid))).astype(BF16)
        agb[chunk, f, :, 2 * hid :] = (grad * swish).astype(BF16)
        for j in range(1, n_f):
            copy_g(k, j).start()

    def products(k):
        values = agb[from_d(k)].reshape(rows, 3 * hid)
        out = dot(values[:, :hid], wd_ref[...], 1, 0)
        back = dot(values[:, hid : 2 * hid], wg_ref[...], 1, 1)
        return out, back + dot(values[:, 2 * hid :], wu_ref[...], 1, 1)

    def copy_h(k):
        return copy(hs.at[k], hr.at[k], sh.at[k], rh.at[k], d_to=from_d(k))

    @pl.loop(1, n_d)
    def _(k):
        for j in range(1, n_f):
            copy_g(k, j).wait_recv()
        out, back = products(k)
        hs[k, 0] = out.astype(BF16)
        hs[k, 1] = back.astype(BF16)
        copy_h(k).start()

    for j in range(1, n_f):
        copy_g(0, j).wait_recv()
    out, back = products(0)
    own[0] = out
    own[1] = back

    def copy_i(j):
        there = at_x(j)
        return copy(isb.at[there], irb.at[xc], si.at[j], ri.at[j], xc_to=there)

    for k in range(1, n_d):
        copy_h(k).wait_recv()
    for a in range(2):
        total = own[a]
        for k in range(1, n_d):
            total = total + hr[k, a].astype(F32)
        isb[:, a] = total.astype(BF16).reshape(n_xc, n_src * CAP, cols)
    irb[xc] = isb[xc]
    for j in range(1, n_xc):
        copy_i(j).start()

    all_values = agb[...].reshape(n_d * rows, 3 * hid)
    gdown_ref[...] = dot(all_values[:, :hid], xe[1].reshape(n_d * rows, cols), 0, 0)

    def copy_k(j):
        there = at_z(j)
        return copy(ks.at[there], kr.at[zl], sk.at[j], rk.at[j], zl_to=there)

    for j in range(1, n_xc):
        copy_i(j).wait_recv()
    returned = irb[:, 0].reshape(slots, cols)
    mixed_part = dot(w_hi[...], returned, 1, 0) + dot(w_lo[...], returned, 1, 0)
    grad_part = dot(w_one[...], irb[:, 1].reshape(slots, cols), 1, 0)
    for a, value in enumerate((mixed_part, grad_part)):
        value = value.reshape(n_zl, n_f * n_tok, cols)
        mp[:, a] = value
        ks[:, a] = value.astype(BF16)
    for j in range(1, n_zl):
        copy_k(j).start()

    ggate_ref[...] = dot(xe[0].reshape(n_d * rows, cols), all_values[:, hid : 2 * hid], 0, 0)

    def copy_l(j):
        there = at_f(j)
        return copy(ls.at[there], lr.at[f], sl.at[j], rl.at[j], f_to=there)

    for j in range(1, n_zl):
        copy_k(j).wait_recv()
    total = mp[zl]
    for j in range(1, n_zl):
        total = total + kr[at_z(j)].astype(F32)
    total = total.astype(BF16)
    for a in range(2):
        ls[:, a] = total[a].reshape(n_f, n_tok, cols)
    lr[f] = ls[f]
    for j in range(1, n_f):
        copy_l(j).start()

    gup_ref[...] = dot(xe[0].reshape(n_d * rows, cols), all_values[:, 2 * hid :], 0, 0)

    for j in range(1, n_f):
        copy_l(j).wait_recv()
    for owner in range(n_f):
        mixed_ref[:, owner * cols : (owner + 1) * cols] = lr[owner, 0]
        gtok_ref[:, owner * cols : (owner + 1) * cols] = lr[owner, 1]

    for j in range(1, n_f):
        copy_ai(j).wait_send()
        copy_l(j).wait_send()
        for a in range(2):
            copy_a(a, j).wait_send()
        for k in range(n_d):
            copy_r(k, j).wait_send()
            copy_g(k, j).wait_send()
    for j in range(1, n_zl):
        copy_bi(j).wait_send()
        copy_k(j).wait_send()
        for a in range(2):
            copy_b(a, j).wait_send()
    for j in range(1, n_xc):
        copy_i(j).wait_send()
        for a in range(2):
            copy_d(a, j).wait_send()
    for j in range(1, n_d):
        copy_h(j).wait_send()
        for a in range(2):
            copy_e(a, j).wait_send()


def body(sizes, tokens, routes, gate_fixed, gate_weight, up_weight, down_weight, cotangent):
    n_zl, n_xc, n_f, n_d = sizes
    n_tok, width = tokens.shape
    cols, hid = gate_weight.shape[1:]
    n_src = n_zl * n_f
    col_tok = n_src * n_tok
    slots = n_xc * n_src * CAP
    rows = slots
    part = rows // n_f
    vmem = pltpu.VMEM
    dma = pltpu.SemaphoreType.DMA
    outs = pl.pallas_call(
        functools.partial(kernel, sizes),
        out_shape=(
            jax.ShapeDtypeStruct((n_tok, width), BF16),
            jax.ShapeDtypeStruct((n_tok, width), BF16),
            jax.ShapeDtypeStruct((hid, cols), F32),
            jax.ShapeDtypeStruct((cols, hid), F32),
            jax.ShapeDtypeStruct((cols, hid), F32),
        ),
        in_specs=[pl.BlockSpec(memory_space=pltpu.VMEM)] * 7,
        out_specs=[pl.BlockSpec(memory_space=pltpu.VMEM)] * 5,
        scratch_shapes=[
            vmem((n_zl, n_f, n_tok, 128), jnp.int32),
            vmem((2, n_zl, n_f, n_tok, cols), BF16),
            vmem((2, n_xc, n_src * CAP, cols), BF16),
            vmem((2, n_d, n_xc, n_src * CAP, cols), BF16),
            vmem((n_d, rows, 3 * hid), F32),
            vmem((n_d, n_f, part, 3 * hid), BF16),
            vmem((n_d, n_f, part, 3 * hid), BF16),
            vmem((n_d, n_f, part, 3 * hid), BF16),
            vmem((n_d, 2, rows, cols), BF16),
            vmem((n_d, 2, rows, cols), BF16),
            vmem((2, rows, cols), F32),
            vmem((n_xc, 2, n_src * CAP, cols), BF16),
            vmem((n_xc, 2, n_src * CAP, cols), BF16),
            vmem((n_zl, 2, n_f * n_tok, cols), F32),
            vmem((n_zl, 2, n_f * n_tok, cols), BF16),
            vmem((n_zl, 2, n_f * n_tok, cols), BF16),
            vmem((n_f, 2, n_tok, cols), BF16),
            vmem((n_f, 2, n_tok, cols), BF16),
            vmem((col_tok, slots), BF16),
            vmem((col_tok, slots), BF16),
            vmem((col_tok, slots), BF16),
        ]
        + [dma((2, n_f)), dma((2, n_f)), dma((n_f,)), dma((n_f,))]
        + [dma((2, n_zl)), dma((2, n_zl)), dma((n_zl,)), dma((n_zl,))]
        + [dma((2, n_xc)), dma((2, n_xc)), dma((2, n_d)), dma((2, n_d))]
        + [dma((n_d, n_f))] * 4
        + [dma((n_d,))] * 2
        + [dma((n_xc,))] * 2
        + [dma((n_zl,))] * 2
        + [dma((n_f,))] * 2,
        compiler_params=pltpu.CompilerParams(
            collective_id=0, has_side_effects=True, vmem_limit_bytes=60 * 1024 * 1024
        ),
    )(tokens, cotangent, routes, gate_fixed, gate_weight[0], up_weight[0], down_weight[0])
    mixed, grad_tokens, grad_down, grad_gate, grad_up = outs
    return mixed, grad_tokens, grad_down[None], grad_gate[None], grad_up[None]


def solution(mesh):
    n_expert, n_f, n_d = (mesh.shape[name] for name in ("expert", "fsdp", "dp"))
    n_zl = 4 if n_expert >= 16 else 2
    sizes = (n_zl, n_expert // n_zl, n_f, n_d)
    tokens = P(("expert", "fsdp", "dp"), None)
    wide = P("expert", "fsdp", "dp")
    tall = P("expert", "dp", "fsdp")
    return jax.shard_map(
        functools.partial(body, sizes),
        mesh=mesh,
        in_specs=(tokens, tokens, tokens, wide, wide, tall, tokens),
        out_specs=(tokens, tokens, tall, wide, wide),
        check_vma=False,
    )
```

time: 715 us -> 299 us (0.42)
  the two profiles are of different devices: /device:TPU:72 before, /device:TPU:109 now
where the time goes in v1:
time: 299 us; the launch traced here: 298 us
  Pallas kernels  289 us (97%)
  local copies, waits for them, and re-layouts  8.95 us (3%)
    pallas_call x1, Pallas kernels, body(): pl.pallas_call(functools.partial(kernel, sizes), out_shape=(jax.ShapeDtyp...  289 us
    unnamed x17, local copies, waits for them, and re-layouts  8.95 us

profile of v1, /device:TPU:109, one launch (start us, length us, event | category | flops | bytes accessed | tf_op | source)
XLA Modules:
  0.0 298.3 jit_solution(492614254469658273)
XLA Ops:
  0.6 0.0 copy-start.3
  0.6 0.7 copy-done.3
  1.3 0.0 copy-start.4
  1.3 0.7 copy.12.routes_ref
  2.0 0.0 copy-done.4
  2.0 0.7 copy.13.fixed_ref
  2.7 288.6 %shard_map.110 = (bf16[16,3584]{1,0:T(8,128)(2,1)}, bf16[16,3584]{1,0:T(8,128)(2,1)}, f32[256,896]{1,0:T(8,128)}, f32[896,256]{1,0:T(8,128)}, f32[896,256]{1,0:T(8,128)}) custom-call(bf16[16,3584]{1,0:T(8,128)(2,1)} %tok_ref.1, bf16[16,3584]{1,0:T(8,128)(2,1)} %cot_ref.1, s32[16,3]{1,0:T(8,128)} %copy.12.routes_ref, s32[16,3]{1,0:T(8,128)} %copy.13.fixed_ref, ...), custom_call_target="tpu_custom_call" | custom-call | tf_op jit(solution)/shard_map/pallas_call | solution.py:342
  291.3 0.0 copy-start.2
  291.3 1.6 copy.19
  292.9 0.0 copy-done.2
  292.9 0.6 copy.20
  293.6 0.0 copy-start.1
  293.6 2.2 copy.21
  295.8 0.0 copy-done.1
  295.8 0.0 copy-start
  295.8 0.9 copy.22
  296.7 0.6 copy-done
  297.3 0.9 copy.23
Async XLA Ops:
  0.6 0.7 copy-start.3
  1.3 0.7 copy-start.4
  291.3 1.6 copy-start.2
  293.6 2.2 copy-start.1
  295.8 1.5 copy-start

commit v2 on v1

v2 whole, which is shorter than its diff:
```python
import functools

import jax
import jax.numpy as jnp
from jax import lax
from jax.experimental import pallas as pl
from jax.experimental.pallas import tpu as pltpu
from jax.sharding import PartitionSpec as P

F32 = jnp.float32
BF16 = jnp.bfloat16
CAP = 2


def log2(number):
    assert number & (number - 1) == 0
    return number.bit_length() - 1


def dot(a, b, ca, cb):
    return lax.dot_general(a, b, (((ca,), (cb,)), ((), ())), preferred_element_type=F32)


def kernel(
    sizes,
    tok_ref, cot_ref, routes_ref, fixed_ref, wg_hbm, wu_hbm, wd_hbm,
    mixed_ref, gtok_ref, gdown_hbm, ggate_hbm, gup_hbm,
    wg_ref, wu_ref, wd_ref, gdown, ggate, gup,
    info, xb, xs, xe, pf, rss, r1, s2, r2, av, hs, hq, hr, own, isb, irb, mp, ks, kr, ls, lr, w_hi, w_lo, w_one,
    local_sem,
    sa, ra, sai, rai, sb, rb, sbi, rbi, sd, rd, se, re, sf, rf, sr, rr, sm, rm, sg, rg, sh, rh, sq, rq,
    si, ri, sk, rk, sl, rl,
):
    n_zl, n_xc, n_f, n_d = sizes
    n_tok, top = routes_ref.shape
    cols = wg_ref.shape[0]
    hid = wg_ref.shape[1]
    n_src = n_zl * n_f
    col_tok = n_src * n_tok
    slots = n_xc * n_src * CAP
    rows = slots
    part = rows // n_f
    half = n_xc // 2

    e = lax.axis_index("expert")
    f = lax.axis_index("fsdp")
    d = lax.axis_index("dp")
    zl = e // n_xc
    xc = e % n_xc

    def at_f(j):
        return (f + j) % n_f

    def at_z(j):
        return (zl + j) % n_zl

    def at_x(j):
        return (xc + j) % n_xc

    def at_d(j):
        return (d + j + n_d) % n_d

    def device(zl_to=zl, xc_to=xc, f_to=f, d_to=d):
        return {"expert": zl_to * n_xc + xc_to, "fsdp": f_to, "dp": d_to}

    sent = []

    def copy(src, dst, send, recv, **to):
        return pltpu.make_async_remote_copy(
            src_ref=src,
            dst_ref=dst,
            send_sem=send,
            recv_sem=recv,
            device_id=device(**to),
            device_id_type=pl.DeviceIdType.MESH,
        )

    def start(one):
        one.start()
        sent.append(one)

    def start_local(source, target, number):
        one = pltpu.make_async_copy(source, target, local_sem.at[number])
        one.start()
        return one

    barrier = pltpu.get_barrier_semaphore()
    count = 0
    for limit, name, at in ((n_f, "f_to", at_f), (n_zl, "zl_to", at_z), (n_xc, "xc_to", at_x), (n_d, "d_to", at_d)):
        for j in range(1, limit):
            pl.semaphore_signal(
                barrier, inc=1, device_id=device(**{name: at(j)}), device_id_type=pl.DeviceIdType.MESH
            )
            count += 1
    weights = [
        start_local(source, target, number)
        for number, (source, target) in enumerate(((wg_hbm, wg_ref), (wu_hbm, wu_ref), (wd_hbm, wd_ref)))
    ]

    lane = lax.broadcasted_iota(jnp.int32, (n_tok, 128), 1)
    packed = jnp.zeros((n_tok, 128), jnp.int32)
    for k in range(top):
        fixed = fixed_ref[:, k : k + 1]
        packed = jnp.where(lane == k, routes_ref[:, k : k + 1], packed)
        packed = jnp.where(lane == top + k, lax.shift_right_logical(fixed, 8), packed)
        packed = jnp.where(lane == 2 * top + k, fixed & 255, packed)
    info[zl, f] = packed.astype(F32).astype(BF16)
    own_cols = pl.ds(pl.multiple_of(f * cols, 128), cols)
    xb[0, zl, f] = tok_ref[:, own_cols]
    xb[1, zl, f] = cot_ref[:, own_cols]

    pl.semaphore_wait(barrier, count)

    def copy_a(a, j):
        there = at_f(j)
        src = (tok_ref, cot_ref)[a]
        columns = pl.ds(pl.multiple_of(there * cols, 128), cols)
        return copy(src.at[:, columns], xb.at[a, zl, f], sa.at[a, j], ra.at[a, j], f_to=there)

    def copy_ai(j):
        return copy(info.at[zl, f], info.at[zl, f], sai.at[j], rai.at[j], f_to=at_f(j))

    for j in range(1, n_f):
        start(copy_ai(j))
    for a in range(2):
        for j in range(1, n_f):
            start(copy_a(a, j))

    def copy_b(a, j):
        return copy(xb.at[a, zl], xb.at[a, zl], sb.at[a, j], rb.at[a, j], zl_to=at_z(j))

    def copy_bi(j):
        return copy(info.at[zl], info.at[zl], sbi.at[j], rbi.at[j], zl_to=at_z(j))

    for j in range(1, n_f):
        copy_ai(j).wait_recv()
    for j in range(1, n_zl):
        start(copy_bi(j))
    for a in range(2):
        for j in range(1, n_f):
            copy_a(a, j).wait_recv()
        for j in range(1, n_zl):
            start(copy_b(a, j))

    for j in range(1, n_zl):
        copy_bi(j).wait_recv()
    table = info[...].reshape(col_tok, 128).astype(F32)
    slot = lax.broadcasted_iota(jnp.int32, (col_tok, slots), 1)
    token = lax.broadcasted_iota(jnp.int32, (col_tok, slots), 0)
    slot_expert = (zl * n_xc + lax.shift_right_logical(slot, log2(n_src * CAP))).astype(F32)
    slot_source = lax.shift_right_logical(slot, log2(CAP)) & (n_src - 1)
    slot_rank = (slot & (CAP - 1)).astype(F32)
    hit = [table[:, k : k + 1] == slot_expert for k in range(top)]
    named = functools.reduce(jnp.logical_or, hit)
    before_row = lax.broadcasted_iota(jnp.int32, (col_tok, col_tok), 0)
    before_col = lax.broadcasted_iota(jnp.int32, (col_tok, col_tok), 1)
    shift = log2(n_tok)
    earlier = (before_col < before_row) & (
        lax.shift_right_logical(before_col, shift) == lax.shift_right_logical(before_row, shift)
    )
    rank = dot(jnp.where(earlier, 1.0, 0.0).astype(BF16), jnp.where(named, 1.0, 0.0).astype(BF16), 1, 0)
    chosen = named & (rank == slot_rank) & (lax.shift_right_logical(token, shift) == slot_source)
    weight = jnp.zeros((col_tok, slots), F32)
    for k in range(top):
        value = table[:, top + k : top + k + 1] * 256.0 + table[:, 2 * top + k : 2 * top + k + 1]
        weight = jnp.where(hit[k], value * (1.0 / 65536.0), weight)
    weight = jnp.where(chosen, weight, 0.0)
    high = weight.astype(BF16)
    w_hi[...] = high
    w_lo[...] = (weight - high.astype(F32)).astype(BF16)
    w_one[...] = jnp.where(chosen, 1.0, 0.0).astype(BF16)

    def copy_d(a, j):
        there = at_x(j)
        return copy(xs.at[a, there], xe.at[a, d, xc], sd.at[a, j], rd.at[a, j], xc_to=there)

    for a in range(2):
        for j in range(1, n_zl):
            copy_b(a, j).wait_recv()
        table_rows = xb[a].reshape(col_tok, cols)
        if a == 0:
            picked = dot(w_one[...], table_rows, 0, 0)
        else:
            picked = dot(w_hi[...], table_rows, 0, 0) + dot(w_lo[...], table_rows, 0, 0)
        xs[a] = picked.astype(BF16).reshape(n_xc, n_src * CAP, cols)
        xe[a, d, xc] = xs[a, xc]
        for j in range(1, n_xc):
            start(copy_d(a, j))

    def from_d(k):
        return at_d(-k)

    def copy_e(a, k):
        return copy(xe.at[a, d], xe.at[a, d], se.at[a, k], re.at[a, k], d_to=at_d(k))

    def copy_far(a, k):
        piece = xe.at[a, from_d(k), pl.ds(0, half) if k == 1 else pl.ds(half, half)]
        return copy(piece, piece, sf.at[a, k], rf.at[a, k], d_to=at_d(k))

    def send_e(a):
        for j in range(1, n_xc):
            copy_d(a, j).wait_recv()
        for k in (1, n_d - 1):
            start(copy_e(a, k))

    def take_e(a, k):
        if k == 2:
            for via in (1, n_d - 1):
                copy_far(a, via).wait_recv()
        elif k != 0:
            copy_e(a, k).wait_recv()
            start(copy_far(a, k))

    def sides(turn):
        step = 1 - 2 * ((f + turn) % 2)
        return (f + step + n_f) % n_f, (f - step + n_f) % n_f

    def sides_r(s, k):
        return sides(s if s < 2 else k % 2)

    def copy_r(s, k, which):
        first, _ = sides_r(s, k)
        quarter = at_f(2) if which == 0 else first
        return copy(
            rss.at[s, k, quarter], r1.at[s, k, quarter], sr.at[s, k, which], rr.at[s, k, which], f_to=first
        )

    def copy_m(s, k):
        _, second = sides_r(s, k)
        return copy(s2.at[s, k], r2.at[s, k], sm.at[s, k], rm.at[s, k], f_to=second)

    def part_of(quarter):
        return pl.ds(pl.multiple_of(quarter * part, part), part)

    def scatter(s, k):
        operand = xe[0 if s < 2 else 1, from_d(k)].reshape(rows, cols)
        product = dot(operand, (wg_ref, wu_ref, wd_ref)[s][...], 1, 0 if s < 2 else 1)
        pf[s, k] = product
        rss[s, k] = product.astype(BF16).reshape(n_f, part, hid)
        for which in range(2):
            start(copy_r(s, k, which))

    def scatter_more(k):
        for s in range(3):
            copy_r(s, k, 0).wait_recv()
            _, second = sides_r(s, k)
            s2[s, k] = (pf[s, k, part_of(second), :] + r1[s, k, second].astype(F32)).astype(BF16)
            start(copy_m(s, k))

    def total_of(s, k):
        copy_r(s, k, 1).wait_recv()
        copy_m(s, k).wait_recv()
        return pf[s, k, part_of(f), :] + r1[s, k, f].astype(F32) + r2[s, k].astype(F32)

    def copy_g(s, k, which):
        first, second = sides(k % 2 if s == 0 else s - 1)
        mine = av.at[s, from_d(k), second if which == 2 else f]
        return copy(mine, mine, sg.at[s, k, which], rg.at[s, k, which], f_to=second if which == 0 else first)

    def gather(k):
        gate = total_of(0, k)
        up = total_of(1, k)
        sigmoid = jax.nn.sigmoid(gate)
        swish = gate * sigmoid
        av[0, from_d(k), f] = (swish * up).astype(BF16)
        for which in range(2):
            start(copy_g(0, k, which))
        grad = total_of(2, k)
        av[1, from_d(k), f] = (grad * up * sigmoid * (1.0 + gate * (1.0 - sigmoid))).astype(BF16)
        av[2, from_d(k), f] = (grad * swish).astype(BF16)
        for which in range(2):
            for s in (1, 2):
                start(copy_g(s, k, which))

    def gather_more(k):
        for s in range(3):
            copy_g(s, k, 0).wait_recv()
            start(copy_g(s, k, 2))

    def copy_h(a, k):
        return copy(hs.at[a, k], hr.at[a, k], sh.at[a, k], rh.at[a, k], d_to=from_d(k))

    def half_of(via):
        return pl.ds(0, half) if via == 1 else pl.ds(half, half)

    def copy_half(a, via):
        return copy(hs.at[a, 2, half_of(via)], hq.at[a, 0 if via == 1 else 1], sh.at[a, 0 if via == 1 else 2],
                    rh.at[a, 0 if via == 1 else 2], d_to=at_d(via))

    def copy_on(a, via):
        number = 0 if via == 1 else 1
        return copy(hq.at[a, number], hr.at[a, 2, half_of(via)], sq.at[a, number], rq.at[a, number], d_to=at_d(via))

    def product_of(a, k):
        for s in (0,) if a == 0 else (1, 2):
            for which in (1, 2):
                copy_g(s, k, which).wait_recv()
        chunk = from_d(k)
        if a == 0:
            return dot(av[0, chunk].reshape(rows, hid), wd_ref[...], 1, 0)
        back = dot(av[1, chunk].reshape(rows, hid), wg_ref[...], 1, 1)
        return back + dot(av[2, chunk].reshape(rows, hid), wu_ref[...], 1, 1)

    def output(a, k):
        hs[a, k] = product_of(a, k).astype(BF16).reshape(n_xc, n_src * CAP, cols)
        if k == 2:
            for via in (1, n_d - 1):
                start(copy_half(a, via))
        else:
            start(copy_h(a, k))

    def pass_on(a):
        for via in (1, n_d - 1):
            copy_half(a, via).wait_recv()
            start(copy_on(a, via))

    def copy_i(a, j):
        there = at_x(j)
        return copy(isb.at[a, there], irb.at[a, xc], si.at[a, j], ri.at[a, j], xc_to=there)

    def send_i(a):
        own[...] = product_of(a, 0)
        for k in (1, n_d - 1):
            copy_h(a, k).wait_recv()
        for via in (1, n_d - 1):
            copy_on(a, via).wait_recv()
        total = own[...].reshape(n_xc, n_src * CAP, cols)
        for k in range(1, n_d):
            total = total + hr[a, k].astype(F32)
        isb[a] = total.astype(BF16)
        irb[a, xc] = isb[a, xc]
        for j in range(1, n_xc):
            start(copy_i(a, j))

    def copy_k(a, j):
        there = at_z(j)
        return copy(ks.at[a, there], kr.at[a, zl], sk.at[a, j], rk.at[a, j], zl_to=there)

    def send_k(a):
        for j in range(1, n_xc):
            copy_i(a, j).wait_recv()
        returned = irb[a].reshape(slots, cols)
        if a == 0:
            value = dot(w_hi[...], returned, 1, 0) + dot(w_lo[...], returned, 1, 0)
        else:
            value = dot(w_one[...], returned, 1, 0)
        value = value.reshape(n_zl, n_f * n_tok, cols)
        mp[a] = value
        ks[a] = value.astype(BF16)
        for j in range(1, n_zl):
            start(copy_k(a, j))

    def copy_l(a, j):
        there = at_f(j)
        return copy(ls.at[a, there], lr.at[a, f], sl.at[a, j], rl.at[a, j], f_to=there)

    def send_l(a):
        for j in range(1, n_zl):
            copy_k(a, j).wait_recv()
        total = mp[a, zl]
        for j in range(1, n_zl):
            total = total + kr[a, at_z(j)].astype(F32)
        ls[a] = total.astype(BF16).reshape(n_f, n_tok, cols)
        lr[a, f] = ls[a, f]
        for j in range(1, n_f):
            start(copy_l(a, j))

    def finish(a):
        for j in range(1, n_f):
            copy_l(a, j).wait_recv()
        for owner in range(n_f):
            (mixed_ref, gtok_ref)[a][:, owner * cols : (owner + 1) * cols] = lr[a, owner]

    for one in weights:
        one.wait()
    send_e(0)
    scatter(0, 0)
    scatter(1, 0)
    send_e(1)
    scatter(2, 0)
    for k, previous in ((1, 0), (3, 1), (2, 3)):
        take_e(0, k)
        scatter(0, k)
        scatter(1, k)
        take_e(1, k)
        scatter(2, k)
        scatter_more(previous)
    gather(1)
    scatter_more(2)
    gather_more(1)
    gather(3)
    gather(2)
    gather_more(3)
    gather(0)
    output(0, 1)
    output(1, 1)
    gather_more(2)
    output(0, 3)
    output(1, 3)
    gather_more(0)
    output(0, 2)
    output(1, 2)
    pass_on(0)
    send_i(0)
    pass_on(1)
    send_i(1)
    all_rows = n_d * rows
    gdown[...] = dot(av[0].reshape(all_rows, hid), xe[1].reshape(all_rows, cols), 0, 0)
    results = [start_local(gdown, gdown_hbm, 0)]
    send_k(0)
    send_k(1)
    ggate[...] = dot(xe[0].reshape(all_rows, cols), av[1].reshape(all_rows, hid), 0, 0)
    results.append(start_local(ggate, ggate_hbm, 1))
    send_l(0)
    send_l(1)
    gup[...] = dot(xe[0].reshape(all_rows, cols), av[2].reshape(all_rows, hid), 0, 0)
    results.append(start_local(gup, gup_hbm, 2))
    finish(0)
    finish(1)
    for one in sent:
        one.wait_send()
    for one in results:
        one.wait()


def body(sizes, tokens, routes, gate_fixed, gate_weight, up_weight, down_weight, cotangent):
    n_zl, n_xc, n_f, n_d = sizes
    n_tok, width = tokens.shape
    cols, hid = gate_weight.shape[1:]
    n_src = n_zl * n_f
    col_tok = n_src * n_tok
    slots = n_xc * n_src * CAP
    rows = slots
    part = rows // n_f
    vmem = pltpu.VMEM
    dma = pltpu.SemaphoreType.DMA
    outs = pl.pallas_call(
        functools.partial(kernel, sizes),
        out_shape=(
            jax.ShapeDtypeStruct((n_tok, width), BF16),
            jax.ShapeDtypeStruct((n_tok, width), BF16),
            jax.ShapeDtypeStruct((hid, cols), F32),
            jax.ShapeDtypeStruct((cols, hid), F32),
            jax.ShapeDtypeStruct((cols, hid), F32),
        ),
        in_specs=[pl.BlockSpec(memory_space=pltpu.VMEM)] * 4 + [pl.BlockSpec(memory_space=pl.ANY)] * 3,
        out_specs=[pl.BlockSpec(memory_space=pltpu.VMEM)] * 2 + [pl.BlockSpec(memory_space=pl.ANY)] * 3,
        scratch_shapes=[
            vmem((cols, hid), BF16),
            vmem((cols, hid), BF16),
            vmem((hid, cols), BF16),
            vmem((hid, cols), F32),
            vmem((cols, hid), F32),
            vmem((cols, hid), F32),
            vmem((n_zl, n_f, n_tok, 128), BF16),
            vmem((2, n_zl, n_f, n_tok, cols), BF16),
            vmem((2, n_xc, n_src * CAP, cols), BF16),
            vmem((2, n_d, n_xc, n_src * CAP, cols), BF16),
            vmem((3, n_d, rows, hid), F32),
            vmem((3, n_d, n_f, part, hid), BF16),
            vmem((3, n_d, n_f, part, hid), BF16),
            vmem((3, n_d, part, hid), BF16),
            vmem((3, n_d, part, hid), BF16),
            vmem((3, n_d, n_f, part, hid), BF16),
            vmem((2, n_d, n_xc, n_src * CAP, cols), BF16),
            vmem((2, 2, n_xc // 2, n_src * CAP, cols), BF16),
            vmem((2, n_d, n_xc, n_src * CAP, cols), BF16),
            vmem((rows, cols), F32),
            vmem((2, n_xc, n_src * CAP, cols), BF16),
            vmem((2, n_xc, n_src * CAP, cols), BF16),
            vmem((2, n_zl, n_f * n_tok, cols), F32),
            vmem((2, n_zl, n_f * n_tok, cols), BF16),
            vmem((2, n_zl, n_f * n_tok, cols), BF16),
            vmem((2, n_f, n_tok, cols), BF16),
            vmem((2, n_f, n_tok, cols), BF16),
            vmem((col_tok, slots), BF16),
            vmem((col_tok, slots), BF16),
            vmem((col_tok, slots), BF16),
            dma((3,)),
        ]
        + [dma((2, n_f)), dma((2, n_f)), dma((n_f,)), dma((n_f,))]
        + [dma((2, n_zl)), dma((2, n_zl)), dma((n_zl,)), dma((n_zl,))]
        + [dma((2, n_xc)), dma((2, n_xc))]
        + [dma((2, n_d))] * 4
        + [dma((3, n_d, 2))] * 2
        + [dma((3, n_d))] * 2
        + [dma((3, n_d, 3))] * 2
        + [dma((2, n_d))] * 2
        + [dma((2, 2))] * 2
        + [dma((2, n_xc))] * 2
        + [dma((2, n_zl))] * 2
        + [dma((2, n_f))] * 2,
        compiler_params=pltpu.CompilerParams(
            collective_id=0, has_side_effects=True, vmem_limit_bytes=60 * 1024 * 1024
        ),
    )(tokens, cotangent, routes, gate_fixed, gate_weight[0], up_weight[0], down_weight[0])
    mixed, grad_tokens, grad_down, grad_gate, grad_up = outs
    return mixed, grad_tokens, grad_down[None], grad_gate[None], grad_up[None]


def solution(mesh):
    n_expert, n_f, n_d = (mesh.shape[name] for name in ("expert", "fsdp", "dp"))
    n_zl = 4 if n_expert >= 16 else 2
    sizes = (n_zl, n_expert // n_zl, n_f, n_d)
    tokens = P(("expert", "fsdp", "dp"), None)
    wide = P("expert", "fsdp", "dp")
    tall = P("expert", "dp", "fsdp")
    return jax.shard_map(
        functools.partial(body, sizes),
        mesh=mesh,
        in_specs=(tokens, tokens, tokens, wide, wide, tall, tokens),
        out_specs=(tokens, tokens, tall, wide, wide),
        check_vma=False,
    )
```

time: 299 us -> 248 us (0.83)
  the two profiles are of different devices: /device:TPU:109 before, /device:TPU:100 now
where the time goes in v2:
time: 248 us
  Pallas kernels  239 us (96%)
  local copies, waits for them, and re-layouts  8.95 us (4%)
    pallas_call x1, Pallas kernels, body(): pl.pallas_call(functools.partial(kernel, sizes), out_shape=(jax.ShapeDtyp...  239 us
    unnamed x17, local copies, waits for them, and re-layouts  8.95 us

profile of v2, /device:TPU:100, one launch (start us, length us, event | category | flops | bytes accessed | tf_op | source)
XLA Modules:
  0.0 248.2 jit_solution(6986460933189231606)
XLA Ops:
  0.6 0.0 copy-start.3
  0.6 0.7 copy-done.3
  1.3 0.0 copy-start.4
  1.3 0.7 copy.12.routes_ref
  2.0 0.0 copy-done.4
  2.0 0.7 copy.13.fixed_ref
  2.7 238.6 %shard_map.110 = (bf16[16,3584]{1,0:T(8,128)(2,1)}, bf16[16,3584]{1,0:T(8,128)(2,1)}, f32[256,896]{1,0:T(8,128)}, f32[896,256]{1,0:T(8,128)}, f32[896,256]{1,0:T(8,128)}) custom-call(bf16[16,3584]{1,0:T(8,128)(2,1)} %tok_ref.1, bf16[16,3584]{1,0:T(8,128)(2,1)} %cot_ref.1, s32[16,3]{1,0:T(8,128)} %copy.12.routes_ref, s32[16,3]{1,0:T(8,128)} %copy.13.fixed_ref, ...), custom_call_target="tpu_custom_call" | custom-call | tf_op jit(solution)/shard_map/pallas_call | solution.py:437
  241.3 0.0 copy-start.2
  241.3 1.6 copy.19
  242.9 0.0 copy-done.2
  242.9 0.6 copy.20
  243.5 0.0 copy-start.1
  243.5 2.2 copy.21
  245.8 0.0 copy-done.1
  245.8 0.0 copy-start
  245.8 0.9 copy.22
  246.7 0.6 copy-done
  247.3 0.9 copy.23
Async XLA Ops:
  0.6 0.7 copy-start.3
  1.3 0.7 copy-start.4
  241.3 1.6 copy-start.2
  243.5 2.2 copy-start.1
  245.8 1.5 copy-start

commit v3 on v2

--- a/solution.py
+++ b/solution.py
@@ -32,7 +32,7 @@
     si, ri, sk, rk, sl, rl,
 ):
     n_zl, n_xc, n_f, n_d = sizes
-    n_tok, top = routes_ref.shape
+    top, n_tok = routes_ref.shape
     cols = wg_ref.shape[0]
     hid = wg_ref.shape[1]
     n_src = n_zl * n_f
@@ -98,13 +98,15 @@
     ]
 
     lane = lax.broadcasted_iota(jnp.int32, (n_tok, 128), 1)
-    packed = jnp.zeros((n_tok, 128), jnp.int32)
-    for k in range(top):
-        fixed = fixed_ref[:, k : k + 1]
-        packed = jnp.where(lane == k, routes_ref[:, k : k + 1], packed)
-        packed = jnp.where(lane == top + k, lax.shift_right_logical(fixed, 8), packed)
-        packed = jnp.where(lane == 2 * top + k, fixed & 255, packed)
-    info[zl, f] = packed.astype(F32).astype(BF16)
+    eye = lax.broadcasted_iota(jnp.int32, (n_tok, n_tok), 0) == lax.broadcasted_iota(jnp.int32, (n_tok, n_tok), 1)
+    chosen_ids, fixed = routes_ref[...], fixed_ref[...]
+    packed = jnp.zeros((n_tok, 128), F32)
+    for number, values in enumerate((chosen_ids, lax.shift_right_logical(fixed, 8), fixed & 255)):
+        values = values.astype(F32)
+        for k in range(top):
+            column = jnp.sum(jnp.where(eye, values[k : k + 1, :], 0.0), axis=1, keepdims=True)
+            packed = jnp.where(lane == number * top + k, column, packed)
+    info[zl, f] = packed.astype(BF16)
     own_cols = pl.ds(pl.multiple_of(f * cols, 128), cols)
     xb[0, zl, f] = tok_ref[:, own_cols]
     xb[1, zl, f] = cot_ref[:, own_cols]
@@ -174,7 +176,7 @@
         there = at_x(j)
         return copy(xs.at[a, there], xe.at[a, d, xc], sd.at[a, j], rd.at[a, j], xc_to=there)
 
-    for a in range(2):
+    def send_d(a):
         for j in range(1, n_zl):
             copy_b(a, j).wait_recv()
         table_rows = xb[a].reshape(col_tok, cols)
@@ -240,12 +242,11 @@
         for which in range(2):
             start(copy_r(s, k, which))
 
-    def scatter_more(k):
-        for s in range(3):
-            copy_r(s, k, 0).wait_recv()
-            _, second = sides_r(s, k)
-            s2[s, k] = (pf[s, k, part_of(second), :] + r1[s, k, second].astype(F32)).astype(BF16)
-            start(copy_m(s, k))
+    def scatter_more(s, k):
+        copy_r(s, k, 0).wait_recv()
+        _, second = sides_r(s, k)
+        s2[s, k] = (pf[s, k, part_of(second), :] + r1[s, k, second].astype(F32)).astype(BF16)
+        start(copy_m(s, k))
 
     def total_of(s, k):
         copy_r(s, k, 1).wait_recv()
@@ -257,23 +258,30 @@
         mine = av.at[s, from_d(k), second if which == 2 else f]
         return copy(mine, mine, sg.at[s, k, which], rg.at[s, k, which], f_to=second if which == 0 else first)
 
-    def gather(k):
-        gate = total_of(0, k)
-        up = total_of(1, k)
+    def activations(k):
+        gate = pf[0, k, part_of(f), :]
         sigmoid = jax.nn.sigmoid(gate)
-        swish = gate * sigmoid
+        return gate, pf[1, k, part_of(f), :], sigmoid, gate * sigmoid
+
+    def gather_hidden(k):
+        for s in range(2):
+            pf[s, k, part_of(f), :] = total_of(s, k)
+        _, up, _, swish = activations(k)
         av[0, from_d(k), f] = (swish * up).astype(BF16)
         for which in range(2):
             start(copy_g(0, k, which))
+
+    def gather_grads(k):
         grad = total_of(2, k)
+        gate, up, sigmoid, swish = activations(k)
         av[1, from_d(k), f] = (grad * up * sigmoid * (1.0 + gate * (1.0 - sigmoid))).astype(BF16)
         av[2, from_d(k), f] = (grad * swish).astype(BF16)
         for which in range(2):
             for s in (1, 2):
                 start(copy_g(s, k, which))
 
-    def gather_more(k):
-        for s in range(3):
+    def gather_more(a, k):
+        for s in (0,) if a == 0 else (1, 2):
             copy_g(s, k, 0).wait_recv()
             start(copy_g(s, k, 2))
 
@@ -371,56 +379,110 @@
         for owner in range(n_f):
             (mixed_ref, gtok_ref)[a][:, owner * cols : (owner + 1) * cols] = lr[a, owner]
 
+    send_d(0)
     for one in weights:
         one.wait()
     send_e(0)
     scatter(0, 0)
     scatter(1, 0)
+    send_d(1)
     send_e(1)
     scatter(2, 0)
-    for k, previous in ((1, 0), (3, 1), (2, 3)):
-        take_e(0, k)
-        scatter(0, k)
-        scatter(1, k)
-        take_e(1, k)
-        scatter(2, k)
-        scatter_more(previous)
-    gather(1)
-    scatter_more(2)
-    gather_more(1)
-    gather(3)
-    gather(2)
-    gather_more(3)
-    gather(0)
+    take_e(0, 1)
+    scatter(0, 1)
+    scatter(1, 1)
+    scatter_more(0, 0)
+    scatter_more(1, 0)
+    take_e(0, 3)
+    scatter(0, 3)
+    scatter(1, 3)
+    take_e(1, 1)
+    scatter(2, 1)
+    scatter_more(2, 0)
+    scatter_more(0, 1)
+    scatter_more(1, 1)
+    take_e(1, 3)
+    scatter(2, 3)
+    take_e(0, 2)
+    scatter(0, 2)
+    scatter(1, 2)
+    scatter_more(2, 1)
+    scatter_more(0, 3)
+    scatter_more(1, 3)
+    take_e(1, 2)
+    scatter(2, 2)
+    scatter_more(2, 3)
+    gather_hidden(1)
+    for s in range(3):
+        scatter_more(s, 2)
+    gather_hidden(3)
+    gather_more(0, 1)
+    gather_hidden(0)
+    gather_hidden(2)
+    gather_more(0, 3)
+    gather_grads(2)
     output(0, 1)
+    gather_more(0, 0)
+    gather_more(0, 2)
+    output(0, 3)
+    gather_grads(1)
+    output(0, 2)
+    gather_more(1, 2)
+    gather_grads(3)
+    pass_on(0)
+    gather_more(1, 1)
+    gather_grads(0)
+    output(1, 2)
+    send_i(0)
+    gather_more(1, 3)
     output(1, 1)
-    gather_more(2)
-    output(0, 3)
+    pass_on(1)
+    gather_more(1, 0)
     output(1, 3)
-    gather_more(0)
-    output(0, 2)
-    output(1, 2)
-    pass_on(0)
-    send_i(0)
-    pass_on(1)
+    send_k(0)
     send_i(1)
     all_rows = n_d * rows
     gdown[...] = dot(av[0].reshape(all_rows, hid), xe[1].reshape(all_rows, cols), 0, 0)
     results = [start_local(gdown, gdown_hbm, 0)]
-    send_k(0)
+    send_l(0)
     send_k(1)
     ggate[...] = dot(xe[0].reshape(all_rows, cols), av[1].reshape(all_rows, hid), 0, 0)
     results.append(start_local(ggate, ggate_hbm, 1))
-    send_l(0)
+    finish(0)
     send_l(1)
     gup[...] = dot(xe[0].reshape(all_rows, cols), av[2].reshape(all_rows, hid), 0, 0)
     results.append(start_local(gup, gup_hbm, 2))
-    finish(0)
     finish(1)
     for one in sent:
         one.wait_send()
     for one in results:
         one.wait()
+
+
+def hand_over_kernel(*refs):
+    count = (len(refs) - 1) // 3
+    sources, targets, held, sem = refs[:count], refs[count : 2 * count], refs[2 * count : 3 * count], refs[-1]
+    into = [pltpu.make_async_copy(sources[i], held[i], sem.at[0, i]) for i in range(count)]
+    out = [pltpu.make_async_copy(held[i], targets[i], sem.at[1, i]) for i in range(count)]
+    for one in into:
+        one.start()
+    for i in range(count):
+        into[i].wait()
+        out[i].start()
+    for one in out:
+        one.wait()
+
+
+def hand_over(arrays):
+    anywhere = pl.BlockSpec(memory_space=pl.ANY)
+    return pl.pallas_call(
+        hand_over_kernel,
+        out_shape=tuple(jax.ShapeDtypeStruct(one.shape, one.dtype) for one in arrays),
+        in_specs=[anywhere] * len(arrays),
+        out_specs=[anywhere] * len(arrays),
+        scratch_shapes=[pltpu.VMEM(one.shape, one.dtype) for one in arrays]
+        + [pltpu.SemaphoreType.DMA((2, len(arrays)))],
+    )(*arrays)
 
 
 def body(sizes, tokens, routes, gate_fixed, gate_weight, up_weight, down_weight, cotangent):
@@ -493,8 +555,8 @@
         compiler_params=pltpu.CompilerParams(
             collective_id=0, has_side_effects=True, vmem_limit_bytes=60 * 1024 * 1024
         ),
-    )(tokens, cotangent, routes, gate_fixed, gate_weight[0], up_weight[0], down_weight[0])
-    mixed, grad_tokens, grad_down, grad_gate, grad_up = outs
+    )(tokens, cotangent, routes.T, gate_fixed.T, gate_weight[0], up_weight[0], down_weight[0])
+    mixed, grad_tokens, grad_down, grad_gate, grad_up = hand_over(outs)
     return mixed, grad_tokens, grad_down[None], grad_gate[None], grad_up[None]
 
 

time: 248 us -> 218 us (0.88)
  the two profiles are of different devices: /device:TPU:100 before, /device:TPU:65 now
where the time goes in v3:
time: 218 us
  Pallas kernels  217 us (100%)
    pallas_call x1, Pallas kernels, body(): pl.pallas_call(functools.partial(kernel, sizes), out_shape=(jax.ShapeDtyp...  214 us

profile of v3, /device:TPU:65, one launch (start us, length us, event | category | flops | bytes accessed | tf_op | source)
XLA Modules:
  0.0 217.7 jit_solution(13821893439951498505)
XLA Ops:
  0.6 214.2 %shard_map.110 = (bf16[16,3584]{1,0:T(8,128)(2,1)}, bf16[16,3584]{1,0:T(8,128)(2,1)}, f32[256,896]{1,0:T(8,128)}, f32[896,256]{1,0:T(8,128)}, f32[896,256]{1,0:T(8,128)}) custom-call(bf16[16,3584]{1,0:T(8,128)(2,1)} %tok_ref.1, bf16[16,3584]{1,0:T(8,128)(2,1)} %cot_ref.1, s32[3,16]{1,0:T(4,128)} %bitcast.11, s32[3,16]{1,0:T(4,128)} %bitcast.12, ...), custom_call_target="tpu_custom_call" | custom-call | tf_op jit(solution)/shard_map/pallas_call | solution.py:499
  214.8 2.9 %shard_map.111 = (bf16[16,3584]{1,0:T(8,128)(2,1)}, bf16[16,3584]{1,0:T(8,128)(2,1)}, f32[256,896]{1,0:T(8,128)}, f32[896,256]{1,0:T(8,128)}, f32[896,256]{1,0:T(8,128)}) custom-call(bf16[16,3584]{1,0:T(8,128)(2,1)} %get-tuple-element.15.refs_0_, bf16[16,3584]{1,0:T(8,128)(2,1)} %get-tuple-element.16.refs_1_, f32[256,896]{1,0:T(8,128)} %get-tuple-element.17.refs_2_, ...), custom_call_target="tpu_custom_call" | custom-call | tf_op jit(solution)/shard_map/pallas_call | solution.py:478

commit v4 on v3

--- a/solution.py
+++ b/solution.py
@@ -26,21 +26,20 @@
     tok_ref, cot_ref, routes_ref, fixed_ref, wg_hbm, wu_hbm, wd_hbm,
     mixed_ref, gtok_ref, gdown_hbm, ggate_hbm, gup_hbm,
     wg_ref, wu_ref, wd_ref, gdown, ggate, gup,
-    info, xb, xs, xe, pf, rss, r1, s2, r2, av, hs, hq, hr, own, isb, irb, mp, ks, kr, ls, lr, w_hi, w_lo, w_one,
+    info, xb, xs, xe, pf, rss, r1, s2, r2, av, tall_send, tall_half, tall_got, wide_send, wide_half, wide_got,
+    own, isb, irb, mp, ks, kr, ls, lr, w_hi, w_lo, w_one,
     local_sem,
     sa, ra, sai, rai, sb, rb, sbi, rbi, sd, rd, se, re, sf, rf, sr, rr, sm, rm, sg, rg, sh, rh, sq, rq,
     si, ri, sk, rk, sl, rl,
 ):
     n_zl, n_xc, n_f, n_d = sizes
     top, n_tok = routes_ref.shape
-    cols = wg_ref.shape[0]
-    hid = wg_ref.shape[1]
+    cols, hid = wg_ref.shape[1:]
     n_src = n_zl * n_f
     col_tok = n_src * n_tok
     slots = n_xc * n_src * CAP
     rows = slots
     part = rows // n_f
-    half = n_xc // 2
 
     e = lax.axis_index("expert")
     f = lax.axis_index("fsdp")
@@ -93,7 +92,7 @@
             )
             count += 1
     weights = [
-        start_local(source, target, number)
+        start_local(source, target.at[0], number)
         for number, (source, target) in enumerate(((wg_hbm, wg_ref), (wu_hbm, wu_ref), (wd_hbm, wd_ref)))
     ]
 
@@ -127,6 +126,33 @@
     for a in range(2):
         for j in range(1, n_f):
             start(copy_a(a, j))
+
+    w_refs = (wg_ref, wu_ref, wd_ref)
+
+    def half_of(rows_of, via):
+        size = rows_of // 2
+        return pl.ds(0, size) if via == 1 else pl.ds(size, size)
+
+    def copy_e(s, k):
+        return copy(w_refs[s].at[0], w_refs[s].at[k], se.at[s, k], re.at[s, k], d_to=at_d(k))
+
+    def copy_far(s, k):
+        piece = half_of(w_refs[s].shape[1], k)
+        return copy(w_refs[s].at[k, piece], w_refs[s].at[2, piece], sf.at[s, k], rf.at[s, k], d_to=at_d(k))
+
+    def pass_weights(s):
+        for k in (1, n_d - 1):
+            copy_e(s, k).wait_recv()
+            start(copy_far(s, k))
+
+    def take_far(s):
+        for k in (1, n_d - 1):
+            copy_far(s, k).wait_recv()
+
+    for s in range(3):
+        weights[s].wait()
+        for k in (1, n_d - 1):
+            start(copy_e(s, k))
 
     def copy_b(a, j):
         return copy(xb.at[a, zl], xb.at[a, zl], sb.at[a, j], rb.at[a, j], zl_to=at_z(j))
@@ -174,7 +200,7 @@
 
     def copy_d(a, j):
         there = at_x(j)
-        return copy(xs.at[a, there], xe.at[a, d, xc], sd.at[a, j], rd.at[a, j], xc_to=there)
+        return copy(xs.at[a, there], xe.at[a, xc], sd.at[a, j], rd.at[a, j], xc_to=there)
 
     def send_d(a):
         for j in range(1, n_zl):
@@ -185,33 +211,13 @@
         else:
             picked = dot(w_hi[...], table_rows, 0, 0) + dot(w_lo[...], table_rows, 0, 0)
         xs[a] = picked.astype(BF16).reshape(n_xc, n_src * CAP, cols)
-        xe[a, d, xc] = xs[a, xc]
+        xe[a, xc] = xs[a, xc]
         for j in range(1, n_xc):
             start(copy_d(a, j))
 
-    def from_d(k):
-        return at_d(-k)
-
-    def copy_e(a, k):
-        return copy(xe.at[a, d], xe.at[a, d], se.at[a, k], re.at[a, k], d_to=at_d(k))
-
-    def copy_far(a, k):
-        piece = xe.at[a, from_d(k), pl.ds(0, half) if k == 1 else pl.ds(half, half)]
-        return copy(piece, piece, sf.at[a, k], rf.at[a, k], d_to=at_d(k))
-
-    def send_e(a):
+    def take_d(a):
         for j in range(1, n_xc):
             copy_d(a, j).wait_recv()
-        for k in (1, n_d - 1):
-            start(copy_e(a, k))
-
-    def take_e(a, k):
-        if k == 2:
-            for via in (1, n_d - 1):
-                copy_far(a, via).wait_recv()
-        elif k != 0:
-            copy_e(a, k).wait_recv()
-            start(copy_far(a, k))
 
     def sides(turn):
         step = 1 - 2 * ((f + turn) % 2)
@@ -235,8 +241,8 @@
         return pl.ds(pl.multiple_of(quarter * part, part), part)
 
     def scatter(s, k):
-        operand = xe[0 if s < 2 else 1, from_d(k)].reshape(rows, cols)
-        product = dot(operand, (wg_ref, wu_ref, wd_ref)[s][...], 1, 0 if s < 2 else 1)
+        operand = xe[0 if s < 2 else 1].reshape(rows, cols)
+        product = dot(operand, w_refs[s][k], 1, 0 if s < 2 else 1)
         pf[s, k] = product
         rss[s, k] = product.astype(BF16).reshape(n_f, part, hid)
         for which in range(2):
@@ -255,7 +261,7 @@
 
     def copy_g(s, k, which):
         first, second = sides(k % 2 if s == 0 else s - 1)
-        mine = av.at[s, from_d(k), second if which == 2 else f]
+        mine = av.at[s, k, second if which == 2 else f]
         return copy(mine, mine, sg.at[s, k, which], rg.at[s, k, which], f_to=second if which == 0 else first)
 
     def activations(k):
@@ -267,15 +273,15 @@
         for s in range(2):
             pf[s, k, part_of(f), :] = total_of(s, k)
         _, up, _, swish = activations(k)
-        av[0, from_d(k), f] = (swish * up).astype(BF16)
+        av[0, k, f] = (swish * up).astype(BF16)
         for which in range(2):
             start(copy_g(0, k, which))
 
     def gather_grads(k):
         grad = total_of(2, k)
         gate, up, sigmoid, swish = activations(k)
-        av[1, from_d(k), f] = (grad * up * sigmoid * (1.0 + gate * (1.0 - sigmoid))).astype(BF16)
-        av[2, from_d(k), f] = (grad * swish).astype(BF16)
+        av[1, k, f] = (grad * up * sigmoid * (1.0 + gate * (1.0 - sigmoid))).astype(BF16)
+        av[2, k, f] = (grad * swish).astype(BF16)
         for which in range(2):
             for s in (1, 2):
                 start(copy_g(s, k, which))
@@ -285,57 +291,78 @@
             copy_g(s, k, 0).wait_recv()
             start(copy_g(s, k, 2))
 
-    def copy_h(a, k):
-        return copy(hs.at[a, k], hr.at[a, k], sh.at[a, k], rh.at[a, k], d_to=from_d(k))
-
-    def half_of(via):
-        return pl.ds(0, half) if via == 1 else pl.ds(half, half)
-
-    def copy_half(a, via):
-        return copy(hs.at[a, 2, half_of(via)], hq.at[a, 0 if via == 1 else 1], sh.at[a, 0 if via == 1 else 2],
-                    rh.at[a, 0 if via == 1 else 2], d_to=at_d(via))
-
-    def copy_on(a, via):
-        number = 0 if via == 1 else 1
-        return copy(hq.at[a, number], hr.at[a, 2, half_of(via)], sq.at[a, number], rq.at[a, number], d_to=at_d(via))
-
-    def product_of(a, k):
+    def gathered(a, k):
         for s in (0,) if a == 0 else (1, 2):
             for which in (1, 2):
                 copy_g(s, k, which).wait_recv()
-        chunk = from_d(k)
+
+    def rows_of(s, k):
+        return av[s, k].reshape(rows, hid)
+
+    def output(a, k, first=False):
+        gathered(a, k)
         if a == 0:
-            return dot(av[0, chunk].reshape(rows, hid), wd_ref[...], 1, 0)
-        back = dot(av[1, chunk].reshape(rows, hid), wg_ref[...], 1, 1)
-        return back + dot(av[2, chunk].reshape(rows, hid), wu_ref[...], 1, 1)
-
-    def output(a, k):
-        hs[a, k] = product_of(a, k).astype(BF16).reshape(n_xc, n_src * CAP, cols)
-        if k == 2:
-            for via in (1, n_d - 1):
-                start(copy_half(a, via))
+            product = dot(rows_of(0, k), wd_ref[k], 1, 0)
         else:
-            start(copy_h(a, k))
-
-    def pass_on(a):
+            product = dot(rows_of(1, k), wg_ref[k], 1, 1) + dot(rows_of(2, k), wu_ref[k], 1, 1)
+        own[a] = product if first else own[a] + product
+
+    grads = (gdown, ggate, gup)
+
+    def buffers_of(s):
+        if s == 0:
+            return tall_send, tall_half, tall_got
+        return wide_send.at[s - 1], wide_half.at[s - 1], wide_got.at[s - 1]
+
+    def weight_grad(s, k):
+        if s == 0:
+            return dot(rows_of(0, k), xe[1].reshape(rows, cols), 0, 0)
+        return dot(xe[0].reshape(rows, cols), rows_of(s, k), 0, 0)
+
+    def copy_half(s, via):
+        source, target, _ = buffers_of(s)
+        piece = half_of(grads[s].shape[0], via)
+        number = 0 if via == 1 else 1
+        return copy(source.at[2, piece], target.at[piece], sq.at[s, number], rq.at[s, number], d_to=at_d(via))
+
+    def copy_h(s, k):
+        source, _, target = buffers_of(s)
+        return copy(source.at[k], target.at[k], sh.at[s, k], rh.at[s, k], d_to=at_d(-k))
+
+    def send_far(s):
+        source, _, _ = buffers_of(s)
+        source[2] = weight_grad(s, 2).astype(BF16)
         for via in (1, n_d - 1):
-            copy_half(a, via).wait_recv()
-            start(copy_on(a, via))
+            start(copy_half(s, via))
+
+    def send_near(s, k):
+        source, joined, _ = buffers_of(s)
+        via = n_d - k
+        term = weight_grad(s, k)
+        size = term.shape[0] // 2
+        copy_half(s, via).wait_recv()
+        if via == 1:
+            source[k, :size] = (term[:size] + joined[:size].astype(F32)).astype(BF16)
+            source[k, size:] = term[size:].astype(BF16)
+        else:
+            source[k, :size] = term[:size].astype(BF16)
+            source[k, size:] = (term[size:] + joined[size:].astype(F32)).astype(BF16)
+        start(copy_h(s, k))
+
+    def keep(s):
+        _, _, got = buffers_of(s)
+        term = weight_grad(s, 0)
+        for k in (1, n_d - 1):
+            copy_h(s, k).wait_recv()
+        grads[s][...] = term + got[1].astype(F32) + got[n_d - 1].astype(F32)
+        return start_local(grads[s], (gdown_hbm, ggate_hbm, gup_hbm)[s], s)
 
     def copy_i(a, j):
         there = at_x(j)
         return copy(isb.at[a, there], irb.at[a, xc], si.at[a, j], ri.at[a, j], xc_to=there)
 
     def send_i(a):
-        own[...] = product_of(a, 0)
-        for k in (1, n_d - 1):
-            copy_h(a, k).wait_recv()
-        for via in (1, n_d - 1):
-            copy_on(a, via).wait_recv()
-        total = own[...].reshape(n_xc, n_src * CAP, cols)
-        for k in range(1, n_d):
-            total = total + hr[a, k].astype(F32)
-        isb[a] = total.astype(BF16)
+        isb[a] = own[a].astype(BF16).reshape(n_xc, n_src * CAP, cols)
         irb[a, xc] = isb[a, xc]
         for j in range(1, n_xc):
             start(copy_i(a, j))
@@ -380,78 +407,81 @@
             (mixed_ref, gtok_ref)[a][:, owner * cols : (owner + 1) * cols] = lr[a, owner]
 
     send_d(0)
-    for one in weights:
-        one.wait()
-    send_e(0)
+    pass_weights(0)
+    take_d(0)
     scatter(0, 0)
     scatter(1, 0)
+    scatter(0, 1)
+    pass_weights(1)
+    scatter(1, 1)
     send_d(1)
-    send_e(1)
-    scatter(2, 0)
-    take_e(0, 1)
-    scatter(0, 1)
-    scatter(1, 1)
+    scatter(0, 3)
+    scatter(1, 3)
     scatter_more(0, 0)
     scatter_more(1, 0)
-    take_e(0, 3)
-    scatter(0, 3)
-    scatter(1, 3)
-    take_e(1, 1)
+    take_d(1)
+    scatter(2, 0)
+    pass_weights(2)
     scatter(2, 1)
-    scatter_more(2, 0)
     scatter_more(0, 1)
     scatter_more(1, 1)
-    take_e(1, 3)
     scatter(2, 3)
-    take_e(0, 2)
+    take_far(0)
     scatter(0, 2)
-    scatter(1, 2)
-    scatter_more(2, 1)
     scatter_more(0, 3)
     scatter_more(1, 3)
-    take_e(1, 2)
+    take_far(1)
+    scatter(1, 2)
+    scatter_more(2, 0)
+    take_far(2)
     scatter(2, 2)
+    scatter_more(2, 1)
+    gather_hidden(0)
     scatter_more(2, 3)
     gather_hidden(1)
     for s in range(3):
         scatter_more(s, 2)
     gather_hidden(3)
+    gather_more(0, 0)
+    gather_hidden(2)
     gather_more(0, 1)
-    gather_hidden(0)
-    gather_hidden(2)
+    gather_grads(2)
     gather_more(0, 3)
-    gather_grads(2)
+    output(0, 0, True)
     output(0, 1)
-    gather_more(0, 0)
+    gather_grads(1)
     gather_more(0, 2)
     output(0, 3)
-    gather_grads(1)
+    gather_grads(3)
+    gather_more(1, 2)
     output(0, 2)
-    gather_more(1, 2)
-    gather_grads(3)
-    pass_on(0)
+    send_i(0)
+    send_far(0)
+    gather_grads(0)
     gather_more(1, 1)
-    gather_grads(0)
-    output(1, 2)
-    send_i(0)
+    output(1, 2, True)
+    send_far(1)
+    send_far(2)
+    send_near(0, 1)
+    send_near(0, 3)
     gather_more(1, 3)
     output(1, 1)
-    pass_on(1)
+    send_near(1, 1)
+    send_near(2, 1)
     gather_more(1, 0)
+    send_k(0)
     output(1, 3)
-    send_k(0)
+    send_near(1, 3)
+    send_near(2, 3)
+    output(1, 0)
     send_i(1)
-    all_rows = n_d * rows
-    gdown[...] = dot(av[0].reshape(all_rows, hid), xe[1].reshape(all_rows, cols), 0, 0)
-    results = [start_local(gdown, gdown_hbm, 0)]
+    results = [keep(0)]
+    send_k(1)
     send_l(0)
-    send_k(1)
-    ggate[...] = dot(xe[0].reshape(all_rows, cols), av[1].reshape(all_rows, hid), 0, 0)
-    results.append(start_local(ggate, ggate_hbm, 1))
+    results.append(keep(1))
+    send_l(1)
+    results.append(keep(2))
     finish(0)
-    send_l(1)
-    gup[...] = dot(xe[0].reshape(all_rows, cols), av[2].reshape(all_rows, hid), 0, 0)
-    results.append(start_local(gup, gup_hbm, 2))
     finish(1)
     for one in sent:
         one.wait_send()
@@ -508,26 +538,29 @@
         in_specs=[pl.BlockSpec(memory_space=pltpu.VMEM)] * 4 + [pl.BlockSpec(memory_space=pl.ANY)] * 3,
         out_specs=[pl.BlockSpec(memory_space=pltpu.VMEM)] * 2 + [pl.BlockSpec(memory_space=pl.ANY)] * 3,
         scratch_shapes=[
-            vmem((cols, hid), BF16),
-            vmem((cols, hid), BF16),
-            vmem((hid, cols), BF16),
+            vmem((n_d, cols, hid), BF16),
+            vmem((n_d, cols, hid), BF16),
+            vmem((n_d, hid, cols), BF16),
             vmem((hid, cols), F32),
             vmem((cols, hid), F32),
             vmem((cols, hid), F32),
             vmem((n_zl, n_f, n_tok, 128), BF16),
             vmem((2, n_zl, n_f, n_tok, cols), BF16),
             vmem((2, n_xc, n_src * CAP, cols), BF16),
-            vmem((2, n_d, n_xc, n_src * CAP, cols), BF16),
+            vmem((2, n_xc, n_src * CAP, cols), BF16),
             vmem((3, n_d, rows, hid), F32),
             vmem((3, n_d, n_f, part, hid), BF16),
             vmem((3, n_d, n_f, part, hid), BF16),
             vmem((3, n_d, part, hid), BF16),
             vmem((3, n_d, part, hid), BF16),
             vmem((3, n_d, n_f, part, hid), BF16),
-            vmem((2, n_d, n_xc, n_src * CAP, cols), BF16),
-            vmem((2, 2, n_xc // 2, n_src * CAP, cols), BF16),
-            vmem((2, n_d, n_xc, n_src * CAP, cols), BF16),
-            vmem((rows, cols), F32),
+            vmem((n_d, hid, cols), BF16),
+            vmem((hid, cols), BF16),
+            vmem((n_d, hid, cols), BF16),
+            vmem((2, n_d, cols, hid), BF16),
+            vmem((2, cols, hid), BF16),
+            vmem((2, n_d, cols, hid), BF16),
+            vmem((2, rows, cols), F32),
             vmem((2, n_xc, n_src * CAP, cols), BF16),
             vmem((2, n_xc, n_src * CAP, cols), BF16),
             vmem((2, n_zl, n_f * n_tok, cols), F32),
@@ -543,12 +576,12 @@
         + [dma((2, n_f)), dma((2, n_f)), dma((n_f,)), dma((n_f,))]
         + [dma((2, n_zl)), dma((2, n_zl)), dma((n_zl,)), dma((n_zl,))]
         + [dma((2, n_xc)), dma((2, n_xc))]
-        + [dma((2, n_d))] * 4
+        + [dma((3, n_d))] * 4
         + [dma((3, n_d, 2))] * 2
         + [dma((3, n_d))] * 2
         + [dma((3, n_d, 3))] * 2
-        + [dma((2, n_d))] * 2
-        + [dma((2, 2))] * 2
+        + [dma((3, n_d))] * 2
+        + [dma((3, 2))] * 2
         + [dma((2, n_xc))] * 2
         + [dma((2, n_zl))] * 2
         + [dma((2, n_f))] * 2,

time: 218 us -> 211 us (0.968)
  the two profiles are of different devices: /device:TPU:65 before, /device:TPU:89 now
where the time goes in v4:
time: 211 us
  Pallas kernels  210 us (100%)
    pallas_call x1, Pallas kernels, body(): pl.pallas_call(functools.partial(kernel, sizes), out_shape=(jax.ShapeDtyp...  207 us

profile of v4, /device:TPU:89, one launch (start us, length us, event | category | flops | bytes accessed | tf_op | source)
XLA Modules:
  0.0 210.8 jit_solution(16315443372848700890)
XLA Ops:
  0.6 207.3 %shard_map.110 = (bf16[16,3584]{1,0:T(8,128)(2,1)}, bf16[16,3584]{1,0:T(8,128)(2,1)}, f32[256,896]{1,0:T(8,128)}, f32[896,256]{1,0:T(8,128)}, f32[896,256]{1,0:T(8,128)}) custom-call(bf16[16,3584]{1,0:T(8,128)(2,1)} %tok_ref.1, bf16[16,3584]{1,0:T(8,128)(2,1)} %cot_ref.1, s32[3,16]{1,0:T(4,128)} %bitcast.11, s32[3,16]{1,0:T(4,128)} %bitcast.12, ...), custom_call_target="tpu_custom_call" | custom-call | tf_op jit(solution)/shard_map/pallas_call | solution.py:529
  207.9 2.9 %shard_map.111 = (bf16[16,3584]{1,0:T(8,128)(2,1)}, bf16[16,3584]{1,0:T(8,128)(2,1)}, f32[256,896]{1,0:T(8,128)}, f32[896,256]{1,0:T(8,128)}, f32[896,256]{1,0:T(8,128)}) custom-call(bf16[16,3584]{1,0:T(8,128)(2,1)} %get-tuple-element.15.refs_0_, bf16[16,3584]{1,0:T(8,128)(2,1)} %get-tuple-element.16.refs_1_, f32[256,896]{1,0:T(8,128)} %get-tuple-element.17.refs_2_, ...), custom_call_target="tpu_custom_call" | custom-call | tf_op jit(solution)/shard_map/pallas_call | solution.py:508
